TPU v7x, 32 devices: a whole 2x2x4 slice. The times are simulated.
32 devices in a mesh: tm: 8 (over z, x), space: 4 (over y, core).
Axes of the slice: x: 2, y: 2, z: 4, core: 2. Of those that a mesh axis runs over, the one named last changes fastest.
Arguments:
- checkpoint: float32 [8, 4, 64, 1024], P('tm', None, 'space'), may hold values from -6 to 6
- advect: float32 [8, 2, 64, 1024], P('tm', None, 'space'), may hold values from -0.2 to 0.2
- diffuse: float32 [8, 64, 1024], P('tm', 'space'), may hold values from 0.1 to 0.2
- obs_rows: int32 [8, 8, 8], P('tm', None, 'space'), may hold values from 0 to 1
- obs_values: float32 [8, 8, 8, 4, 8, 1024], P('tm', None, 'space'), may hold values from -6 to 6
- obs_weight: float32 [8], P('tm'), may hold values from 0.5 to 13.5
- error_inverse: float32 [8, 4], P('tm'), may hold values from 0.3 to 3
- rates: float32 [8, 4], replicated, may hold values from 0.07924466 to 1, as said below
Outputs:
- direction: float32 [8, 4, 64, 1024], P('tm', None, 'space')
- grad_rms: float32 [], replicated
Inputs may be any that keep to these rules, and one draw needn't show every extreme that they name: `obs_rows`: entry i of the last dimension counts blocks of 8 rows within the rows of space block i // 2; repeats may occur. `rates`: every entry is below 1.
All inputs are finite; a program needn't handle non-finite values.
Results may differ from a plain program's by a relative error of at most 0.0003.
Values sent between devices are 32-bit elements; how exact they have to be, the bound alone decides.
A program may use at most 64 MiB of HBM per device.

v0:
```python
import jax
import jax.numpy as jnp
from jax import lax
from jax.sharding import PartitionSpec as P

STEPS = 8
BLOCK = 8


def padded_2(block, sides, width):
    for axis, dim in sides:
        count = lax.axis_size(axis)
        forward = [(i, i + 1) for i in range(count - 1)]
        backward = [(target, source) for source, target in forward]
        low = lax.ppermute(
            lax.slice_in_dim(block, block.shape[dim] - width, None, axis=dim), axis, forward
        )
        high = lax.ppermute(lax.slice_in_dim(block, 0, width, axis=dim), axis, backward)
        block = jnp.concatenate([low, block, high], axis=dim)
    return block


def passed_along(value, axis, steps):
    count = lax.axis_size(axis)
    leading, last = (max(0, -steps), min(count, count - steps))
    return lax.ppermute(value, axis, [(source, source + steps) for source in range(leading, last)])


def stencil_of(advect_one, diffuse_one):
    centre = 1.0 - 4.0 * diffuse_one
    to_east = diffuse_one - 0.5 * advect_one[0]
    to_west = diffuse_one + 0.5 * advect_one[0]
    to_north = diffuse_one - 0.5 * advect_one[1]
    to_south = diffuse_one + 0.5 * advect_one[1]
    return (centre, to_east, to_west, to_north, to_south)


def advance(field_now, stencil):
    centre, to_east, to_west, to_north, to_south = stencil
    padded = padded_2(field_now, (("space", 1),), 1)
    return (
        centre * field_now
        + to_east * jnp.roll(field_now, -1, axis=2)
        + to_west * jnp.roll(field_now, 1, axis=2)
        + to_north * padded[:, 2:]
        + to_south * padded[:, :-2]
    )


def retreat(costate, stencil, north_pad, south_pad):
    padded = padded_2(costate, (("space", 1),), 1)
    centre, to_east, to_west = (stencil[0], stencil[1], stencil[2])
    return (
        centre * costate
        + jnp.roll(to_east * costate, 1, axis=2)
        + jnp.roll(to_west * costate, -1, axis=2)
        + (north_pad * padded)[:, :-2]
        + (south_pad * padded)[:, 2:]
    )


def select_rows(field_now, picker):
    blocks = field_now.reshape(field_now.shape[0], picker.shape[1], BLOCK, field_now.shape[2])
    return jnp.einsum("kb,cbrx->kcrx", picker, blocks, precision=lax.Precision.HIGHEST)


def spread_rows(misfit, picker, field_shape):
    placed = jnp.einsum("kb,kcrx->cbrx", picker, misfit, precision=lax.Precision.HIGHEST)
    return placed.reshape(field_shape)


def weigh_own(field_now, initial, inverse_row):
    prior_end = passed_along(field_now, "tm", 1)
    return inverse_row[:, None, None] * (initial - prior_end)


def adjoint_sweep(misfits, pickers, weight, later_term, stencil, north_pad, south_pad, field_shape):
    costate = spread_rows(weight * misfits[STEPS - 1], pickers[STEPS - 1], field_shape) - later_term
    for moment in range(STEPS, 0, -1):
        costate = retreat(costate, stencil, north_pad, south_pad)
        if moment >= 2:
            costate = costate + spread_rows(
                weight * misfits[moment - 2], pickers[moment - 2], field_shape
            )
    return costate


def combine(earlier, latter):
    return (earlier[0] * latter[0], latter[0] * earlier[1] + latter[1])


def on_device(checkpoint, advect, diffuse, obs_rows, obs_values, obs_weight, error_inverse, rates):
    initial = checkpoint[0]
    field_shape = initial.shape
    stencil = stencil_of(advect[0], diffuse[0])
    rim_coefs = padded_2(jnp.stack([advect[0, 1], diffuse[0]]), (("space", 1),), 1)
    north_pad = rim_coefs[1] - 0.5 * rim_coefs[0]
    south_pad = rim_coefs[1] + 0.5 * rim_coefs[0]
    block_count = field_shape[1] // BLOCK
    block_ids = jnp.arange(block_count, dtype=jnp.int32)
    pickers = [
        (obs_rows[0, moment][:, None] == block_ids[None, :]).astype(jnp.float32)
        for moment in range(STEPS)
    ]
    field_now = initial
    misfits = []
    for moment in range(STEPS):
        field_now = advance(field_now, stencil)
        misfits.append(select_rows(field_now, pickers[moment]) - obs_values[0, moment])
    weight = obs_weight[0]
    weighted = weigh_own(field_now, initial, error_inverse[0])
    later_term = passed_along(weighted, "tm", -1)
    costate = adjoint_sweep(
        misfits, pickers, weight, later_term, stencil, north_pad, south_pad, field_shape
    )
    gradient = costate + weighted
    square_sum = lax.psum(jnp.sum(gradient * gradient), ("tm", "space"))
    entries = lax.axis_size("tm") * lax.axis_size("space") * gradient.size
    rms_value = jnp.sqrt(square_sum / entries + 1e-06)
    position = lax.axis_index("tm")
    windows = lax.axis_size("tm")
    innovation = jnp.sqrt(1.0 - rates * rates)
    next_rates = jnp.concatenate([rates[1:], jnp.zeros((1, rates.shape[1]), jnp.float32)], axis=0)
    column_count = gradient.size // windows
    flat_grad = gradient.reshape(1, gradient.size)
    columns = lax.all_to_all(flat_grad, "tm", split_axis=1, concat_axis=0, tiled=True)
    places = position * column_count + jnp.arange(column_count, dtype=jnp.int32)
    member = places // (field_shape[1] * field_shape[2])
    onehot = (member[None, :] == jnp.arange(field_shape[0], dtype=jnp.int32)[:, None]).astype(
        jnp.float32
    )
    rate_cols = jnp.dot(rates, onehot, precision=lax.Precision.HIGHEST)
    inno_cols = jnp.dot(innovation, onehot, precision=lax.Precision.HIGHEST)
    next_cols = jnp.dot(next_rates, onehot, precision=lax.Precision.HIGHEST)
    forward_cols = lax.associative_scan(combine, (rate_cols, inno_cols * columns), axis=0)[1]
    backward_cols = lax.associative_scan(
        combine, (next_cols, inno_cols * forward_cols), reverse=True, axis=0
    )[1]
    flat_back = lax.all_to_all(backward_cols, "tm", split_axis=0, concat_axis=1, tiled=True)
    smoothed = flat_back.reshape(field_shape)
    direction = (smoothed / rms_value)[None]
    return (direction, rms_value)


def solution(mesh):
    placed = (
        P("tm", None, "space", None),
        P("tm", None, "space", None),
        P("tm", "space", None),
        P("tm", None, "space"),
        P("tm", None, "space", None, None, None),
        P("tm"),
        P("tm", None),
        P(),
    )
    return jax.shard_map(
        on_device,
        mesh=mesh,
        in_specs=placed,
        out_specs=(P("tm", None, "space", None), P()),
        check_vma=False,
    )
```

profile of v0, /device:TPU:0, one launch (start us, length us, event | category | flops | bytes accessed | tf_op | source)
XLA Modules:
  0.0 239.0 jit_solution(10749359197541015536)
XLA Ops:
  1.6 2.4 %collective-permute-start.1 = (f32[4,1,1024]{2,1,0:T(1,128)S(1)}, f32[4,1,1024]{2,1,0:T(1,128)S(1)}, u32[]{:S(2)}, u32[]{:S(2)}) collective-permute-start(f32[4,1,1024]{2,1,0:T(1,128)S(1)} %get-tuple-element.99), channel_id=1, source_target_pairs={{0,1},{1,2},{2,3},{4,5},{5,6},{6,7},{8,9},{9,10},{10,11},{12,13},{... | collective-permute-start | bytes 49160 | tf_op jit(solution)/shard_map/ppermute | solution.py:15
  4.0 1.3 collective-permute-start
  7.0 1.3 collective-permute-start.19
  8.3 5.8 %collective-permute-start.18 = (f32[2,1,1024]{2,1,0:T(1,128)S(1)}, f32[2,1,1024]{2,1,0:T(1,128)S(1)}, u32[]{:S(2)}, u32[]{:S(2)}) collective-permute-start(f32[2,1,1024]{2,1,0:T(1,128)S(1)} %get-tuple-element.114), channel_id=1, source_target_pairs={{0,1},{1,2},{2,3},{4,5},{5,6},{6,7},{8,9},{9,10},{10,11},{12,13},{... | collective-permute-start | bytes 24584 | tf_op jit(solution)/shard_map/ppermute | solution.py:15
  17.1 1.7 fusion.161
  20.3 3.6 %collective-permute-start.3 = (f32[4,1,1024]{2,1,0:T(1,128)S(1)}, f32[4,1,1024]{2,1,0:T(1,128)S(1)}, u32[]{:S(2)}, u32[]{:S(2)}) collective-permute-start(f32[4,1,1024]{2,1,0:T(1,128)S(1)} %get-tuple-element.93), channel_id=1, source_target_pairs={{0,1},{1,2},{2,3},{4,5},{5,6},{6,7},{8,9},{9,10},{10,11},{12,13},{... | collective-permute-start | bytes 49160 | tf_op jit(solution)/shard_map/ppermute | solution.py:15
  24.0 1.3 collective-permute-start.2
  27.4 4.4 %collective-permute-start.5 = (f32[4,1,1024]{2,1,0:T(1,128)S(1)}, f32[4,1,1024]{2,1,0:T(1,128)S(1)}, u32[]{:S(2)}, u32[]{:S(2)}) collective-permute-start(f32[4,1,1024]{2,1,0:T(1,128)S(1)} %get-tuple-element.87), channel_id=1, source_target_pairs={{0,1},{1,2},{2,3},{4,5},{5,6},{6,7},{8,9},{9,10},{10,11},{12,13},{... | collective-permute-start | bytes 49160 | tf_op jit(solution)/shard_map/ppermute | solution.py:15
  31.8 1.3 collective-permute-start.4
  35.2 4.2 %collective-permute-start.7 = (f32[4,1,1024]{2,1,0:T(1,128)S(1)}, f32[4,1,1024]{2,1,0:T(1,128)S(1)}, u32[]{:S(2)}, u32[]{:S(2)}) collective-permute-start(f32[4,1,1024]{2,1,0:T(1,128)S(1)} %get-tuple-element.81), channel_id=1, source_target_pairs={{0,1},{1,2},{2,3},{4,5},{5,6},{6,7},{8,9},{9,10},{10,11},{12,13},{... | collective-permute-start | bytes 49160 | tf_op jit(solution)/shard_map/ppermute | solution.py:15
  39.4 1.3 collective-permute-start.6
  42.8 4.2 %collective-permute-start.9 = (f32[4,1,1024]{2,1,0:T(1,128)S(1)}, f32[4,1,1024]{2,1,0:T(1,128)S(1)}, u32[]{:S(2)}, u32[]{:S(2)}) collective-permute-start(f32[4,1,1024]{2,1,0:T(1,128)S(1)} %get-tuple-element.75), channel_id=1, source_target_pairs={{0,1},{1,2},{2,3},{4,5},{5,6},{6,7},{8,9},{9,10},{10,11},{12,13},{... | collective-permute-start | bytes 49160 | tf_op jit(solution)/shard_map/ppermute | solution.py:15
  46.9 1.3 collective-permute-start.8
  50.4 4.2 %collective-permute-start.11 = (f32[4,1,1024]{2,1,0:T(1,128)S(1)}, f32[4,1,1024]{2,1,0:T(1,128)S(1)}, u32[]{:S(2)}, u32[]{:S(2)}) collective-permute-start(f32[4,1,1024]{2,1,0:T(1,128)S(1)} %get-tuple-element.69), channel_id=1, source_target_pairs={{0,1},{1,2},{2,3},{4,5},{5,6},{6,7},{8,9},{9,10},{10,11},{12,13},{... | collective-permute-start | bytes 49160 | tf_op jit(solution)/shard_map/ppermute | solution.py:15
  54.5 1.3 collective-permute-start.10
  57.9 4.2 %collective-permute-start.13 = (f32[4,1,1024]{2,1,0:T(1,128)S(1)}, f32[4,1,1024]{2,1,0:T(1,128)S(1)}, u32[]{:S(2)}, u32[]{:S(2)}) collective-permute-start(f32[4,1,1024]{2,1,0:T(1,128)S(1)} %get-tuple-element.63), channel_id=1, source_target_pairs={{0,1},{1,2},{2,3},{4,5},{5,6},{6,7},{8,9},{9,10},{10,11},{12,13},{... | collective-permute-start | bytes 49160 | tf_op jit(solution)/shard_map/ppermute | solution.py:15
  62.1 1.5 collective-permute-start.12
  65.6 4.1 %collective-permute-start.15 = (f32[4,1,1024]{2,1,0:T(1,128)S(1)}, f32[4,1,1024]{2,1,0:T(1,128)S(1)}, u32[]{:S(2)}, u32[]{:S(2)}) collective-permute-start(f32[4,1,1024]{2,1,0:T(1,128)S(1)} %get-tuple-element.57), channel_id=1, source_target_pairs={{0,1},{1,2},{2,3},{4,5},{5,6},{6,7},{8,9},{9,10},{10,11},{12,13},{... | collective-permute-start | bytes 49160 | tf_op jit(solution)/shard_map/ppermute | solution.py:15
  69.7 1.3 collective-permute-start.14
  71.1 1.7 collective-permute-done.14
  73.0 3.4 %collective-permute-start.16 = (f32[4,16,1024]{2,1,0:T(8,128)S(1)}, f32[4,16,1024]{2,1,0:T(8,128)S(1)}, u32[]{:S(2)}, u32[]{:S(2)}) collective-permute-start(f32[4,16,1024]{2,1,0:T(8,128)S(1)} %fusion.33), channel_id=1, source_target_pairs={{0,4},{4,8},{8,12},{12,16},{16,20},{20,24},{24,28},{1,5},{5,9},{9,... | collective-permute-start | bytes 786440 | tf_op jit(solution)/shard_map/ppermute | solution.py:26
  78.0 3.6 %collective-permute-done.16 = f32[4,16,1024]{2,1,0:T(8,128)S(1)} collective-permute-done((f32[4,16,1024]{2,1,0:T(8,128)S(1)}, f32[4,16,1024]{2,1,0:T(8,128)S(1)}, u32[]{:S(2)}, u32[]{:S(2)}) %collective-permute-start.16) | collective-permute-done | bytes 262176 | tf_op jit(solution)/shard_map/ppermute | solution.py:26
  81.7 1.3 collective-permute-start.17
  84.6 8.1 %collective-permute-done.17 = f32[4,16,1024]{2,1,0:T(8,128)S(1)} collective-permute-done((f32[4,16,1024]{2,1,0:T(8,128)S(1)}, f32[4,16,1024]{2,1,0:T(8,128)S(1)}, u32[]{:S(2)}, u32[]{:S(2)}) %collective-permute-start.17) | collective-permute-done | bytes 262176 | tf_op jit(solution)/shard_map/ppermute | solution.py:26
  92.8 1.3 collective-permute-start.21
  94.1 3.0 %collective-permute-start.20 = (f32[4,1,1024]{2,1,0:T(1,128)S(1)}, f32[4,1,1024]{2,1,0:T(1,128)S(1)}, u32[]{:S(2)}, u32[]{:S(2)}) collective-permute-start(f32[4,1,1024]{2,1,0:T(1,128)S(1)} %get-tuple-element.50), channel_id=1, source_target_pairs={{0,1},{1,2},{2,3},{4,5},{5,6},{6,7},{8,9},{9,10},{10,11},{12,13},{... | collective-permute-start | bytes 49160 | tf_op jit(solution)/shard_map/ppermute | solution.py:15
  98.3 1.3 collective-permute-start.23
  99.6 4.2 %collective-permute-start.22 = (f32[4,1,1024]{2,1,0:T(1,128)S(1)}, f32[4,1,1024]{2,1,0:T(1,128)S(1)}, u32[]{:S(2)}, u32[]{:S(2)}) collective-permute-start(f32[4,1,1024]{2,1,0:T(1,128)S(1)} %get-tuple-element.48), channel_id=1, source_target_pairs={{0,1},{1,2},{2,3},{4,5},{5,6},{6,7},{8,9},{9,10},{10,11},{12,13},{... | collective-permute-start | bytes 49160 | tf_op jit(solution)/shard_map/ppermute | solution.py:15
  105.0 1.3 collective-permute-start.25
  106.3 4.9 %collective-permute-start.24 = (f32[4,1,1024]{2,1,0:T(1,128)S(1)}, f32[4,1,1024]{2,1,0:T(1,128)S(1)}, u32[]{:S(2)}, u32[]{:S(2)}) collective-permute-start(f32[4,1,1024]{2,1,0:T(1,128)S(1)} %get-tuple-element.46), channel_id=1, source_target_pairs={{0,1},{1,2},{2,3},{4,5},{5,6},{6,7},{8,9},{9,10},{10,11},{12,13},{... | collective-permute-start | bytes 49160 | tf_op jit(solution)/shard_map/ppermute | solution.py:15
  112.3 1.3 collective-permute-start.27
  113.6 4.9 %collective-permute-start.26 = (f32[4,1,1024]{2,1,0:T(1,128)S(1)}, f32[4,1,1024]{2,1,0:T(1,128)S(1)}, u32[]{:S(2)}, u32[]{:S(2)}) collective-permute-start(f32[4,1,1024]{2,1,0:T(1,128)S(1)} %get-tuple-element.44), channel_id=1, source_target_pairs={{0,1},{1,2},{2,3},{4,5},{5,6},{6,7},{8,9},{9,10},{10,11},{12,13},{... | collective-permute-start | bytes 49160 | tf_op jit(solution)/shard_map/ppermute | solution.py:15
  119.6 1.3 collective-permute-start.29
  120.9 4.9 %collective-permute-start.28 = (f32[4,1,1024]{2,1,0:T(1,128)S(1)}, f32[4,1,1024]{2,1,0:T(1,128)S(1)}, u32[]{:S(2)}, u32[]{:S(2)}) collective-permute-start(f32[4,1,1024]{2,1,0:T(1,128)S(1)} %get-tuple-element.42), channel_id=1, source_target_pairs={{0,1},{1,2},{2,3},{4,5},{5,6},{6,7},{8,9},{9,10},{10,11},{12,13},{... | collective-permute-start | bytes 49160 | tf_op jit(solution)/shard_map/ppermute | solution.py:15
  127.0 1.3 collective-permute-start.31
  128.3 4.9 %collective-permute-start.30 = (f32[4,1,1024]{2,1,0:T(1,128)S(1)}, f32[4,1,1024]{2,1,0:T(1,128)S(1)}, u32[]{:S(2)}, u32[]{:S(2)}) collective-permute-start(f32[4,1,1024]{2,1,0:T(1,128)S(1)} %get-tuple-element.40), channel_id=1, source_target_pairs={{0,1},{1,2},{2,3},{4,5},{5,6},{6,7},{8,9},{9,10},{10,11},{12,13},{... | collective-permute-start | bytes 49160 | tf_op jit(solution)/shard_map/ppermute | solution.py:15
  134.3 1.3 collective-permute-start.33
  135.6 4.9 %collective-permute-start.32 = (f32[4,1,1024]{2,1,0:T(1,128)S(1)}, f32[4,1,1024]{2,1,0:T(1,128)S(1)}, u32[]{:S(2)}, u32[]{:S(2)}) collective-permute-start(f32[4,1,1024]{2,1,0:T(1,128)S(1)} %get-tuple-element.38), channel_id=1, source_target_pairs={{0,1},{1,2},{2,3},{4,5},{5,6},{6,7},{8,9},{9,10},{10,11},{12,13},{... | collective-permute-start | bytes 49160 | tf_op jit(solution)/shard_map/ppermute | solution.py:15
  142.9 4.9 %collective-permute-start.34 = (f32[4,1,1024]{2,1,0:T(1,128)S(1)}, f32[4,1,1024]{2,1,0:T(1,128)S(1)}, u32[]{:S(2)}, u32[]{:S(2)}) collective-permute-start(f32[4,1,1024]{2,1,0:T(1,128)S(1)} %get-tuple-element.36), channel_id=1, source_target_pairs={{0,1},{1,2},{2,3},{4,5},{5,6},{6,7},{8,9},{9,10},{10,11},{12,13},{... | collective-permute-start | bytes 49160 | tf_op jit(solution)/shard_map/ppermute | solution.py:15
  150.5 6.3 %all-to-all-start = ((f32[1,8,8192]{2,0,1:T(1,128)}), f32[1,8,8192]{2,0,1:T(1,128)S(1)}, u32[]{:S(2)}, u32[]{:S(2)}) async-start(f32[1,8,8192]{2,0,1:T(1,128)} %all_to_all.27), calls=%async_computation | async-start | bytes 524288 | tf_op jit(solution)/shard_map/all_to_all | solution.py:126
  162.4 1.6 slice.797
  164.0 1.6 slice.806
  165.5 1.6 slice.799
  175.8 1.6 slice.803
  177.4 1.6 slice.801
  181.7 1.6 slice.819
  185.9 6.0 %all-to-all-start.1 = ((f32[8,1,8192]{2,1,0:T(1,128)}), f32[8,1,8192]{2,1,0:T(1,128)S(1)}, u32[]{:S(2)}, u32[]{:S(2)}) async-start(f32[8,1,8192]{2,1,0:T(1,128)} %copy.67), calls=%async_computation.1 | async-start | bytes 524288 | tf_op jit(solution)/shard_map/all_to_all | solution.py:139
  191.9 43.9 %psum.7 = f32[]{:T(128)} all-reduce(f32[]{:T(128)} %get-tuple-element.10), channel_id=1, replica_groups=mesh['tm'=8,'space'=4] {'tm','space'}, use_global_device_ids=true, to_apply=%region_1.2 | all-reduce | flops 1 | bytes 8 | tf_op jit(solution)/shard_map/psum | solution.py:117
  (220 shorter events, 55.0 us)
Async XLA Ops:
  1.6 18.3 %collective-permute-start.1 = (f32[4,1,1024]{2,1,0:T(1,128)S(1)}, f32[4,1,1024]{2,1,0:T(1,128)S(1)}, u32[]{:S(2)}, u32[]{:S(2)}) collective-permute-start(f32[4,1,1024]{2,1,0:T(1,128)S(1)} %get-tuple-element.99), channel_id=1, source_target_pairs={{0,1},{1,2},{2,3},{4,5},{5,6},{6,7},{8,9},{9,10},{10,11},{12,13},{... | collective-permute-start | bytes 49160 | tf_op jit(solution)/shard_map/ppermute | solution.py:15
  4.0 15.9 %collective-permute-start = (f32[4,1,1024]{2,1,0:T(1,128)S(1)}, f32[4,1,1024]{2,1,0:T(1,128)S(1)}, u32[]{:S(2)}, u32[]{:S(2)}) collective-permute-start(f32[4,1,1024]{2,1,0:T(1,128)S(1)} %get-tuple-element.98), channel_id=1, source_target_pairs={{1,0},{2,1},{3,2},{5,4},{6,5},{7,6},{9,8},{10,9},{11,10},{13,12},{... | collective-permute-start | bytes 49160 | tf_op jit(solution)/shard_map/ppermute | solution.py:18
  7.0 12.8 %collective-permute-start.19 = (f32[2,1,1024]{2,1,0:T(1,128)S(1)}, f32[2,1,1024]{2,1,0:T(1,128)S(1)}, u32[]{:S(2)}, u32[]{:S(2)}) collective-permute-start(f32[2,1,1024]{2,1,0:T(1,128)S(1)} %get-tuple-element.115), channel_id=1, source_target_pairs={{1,0},{2,1},{3,2},{5,4},{6,5},{7,6},{9,8},{10,9},{11,10},{13,12},{... | collective-permute-start | bytes 24584 | tf_op jit(solution)/shard_map/ppermute | solution.py:18
  8.3 11.5 %collective-permute-start.18 = (f32[2,1,1024]{2,1,0:T(1,128)S(1)}, f32[2,1,1024]{2,1,0:T(1,128)S(1)}, u32[]{:S(2)}, u32[]{:S(2)}) collective-permute-start(f32[2,1,1024]{2,1,0:T(1,128)S(1)} %get-tuple-element.114), channel_id=1, source_target_pairs={{0,1},{1,2},{2,3},{4,5},{5,6},{6,7},{8,9},{9,10},{10,11},{12,13},{... | collective-permute-start | bytes 24584 | tf_op jit(solution)/shard_map/ppermute | solution.py:15
  17.1 1.8 copy-start.2
  17.1 2.7 %copy-start.1 = (f32[1,16,1024]{2,1,0:T(8,128)S(1)}, f32[1,16,1024]{2,1,0:T(8,128)}, u32[]{:S(2)}) copy-start(f32[1,16,1024]{2,1,0:T(8,128)} %param.10) | copy-start | bytes 196612
  17.1 2.9 %copy-start = (f32[1,4,16,1024]{3,2,1,0:T(8,128)S(1)}, f32[1,4,16,1024]{3,2,1,0:T(8,128)}, u32[]{:S(2)}) copy-start(f32[1,4,16,1024]{3,2,1,0:T(8,128)} %param.8) | copy-start | bytes 786436
  20.3 6.6 %collective-permute-start.3 = (f32[4,1,1024]{2,1,0:T(1,128)S(1)}, f32[4,1,1024]{2,1,0:T(1,128)S(1)}, u32[]{:S(2)}, u32[]{:S(2)}) collective-permute-start(f32[4,1,1024]{2,1,0:T(1,128)S(1)} %get-tuple-element.93), channel_id=1, source_target_pairs={{0,1},{1,2},{2,3},{4,5},{5,6},{6,7},{8,9},{9,10},{10,11},{12,13},{... | collective-permute-start | bytes 49160 | tf_op jit(solution)/shard_map/ppermute | solution.py:15
  24.0 3.1 %collective-permute-start.2 = (f32[4,1,1024]{2,1,0:T(1,128)S(1)}, f32[4,1,1024]{2,1,0:T(1,128)S(1)}, u32[]{:S(2)}, u32[]{:S(2)}) collective-permute-start(f32[4,1,1024]{2,1,0:T(1,128)S(1)} %get-tuple-element.92), channel_id=1, source_target_pairs={{1,0},{2,1},{3,2},{5,4},{6,5},{7,6},{9,8},{10,9},{11,10},{13,12},{... | collective-permute-start | bytes 49160 | tf_op jit(solution)/shard_map/ppermute | solution.py:18
  27.4 7.3 %collective-permute-start.5 = (f32[4,1,1024]{2,1,0:T(1,128)S(1)}, f32[4,1,1024]{2,1,0:T(1,128)S(1)}, u32[]{:S(2)}, u32[]{:S(2)}) collective-permute-start(f32[4,1,1024]{2,1,0:T(1,128)S(1)} %get-tuple-element.87), channel_id=1, source_target_pairs={{0,1},{1,2},{2,3},{4,5},{5,6},{6,7},{8,9},{9,10},{10,11},{12,13},{... | collective-permute-start | bytes 49160 | tf_op jit(solution)/shard_map/ppermute | solution.py:15
  31.8 3.1 %collective-permute-start.4 = (f32[4,1,1024]{2,1,0:T(1,128)S(1)}, f32[4,1,1024]{2,1,0:T(1,128)S(1)}, u32[]{:S(2)}, u32[]{:S(2)}) collective-permute-start(f32[4,1,1024]{2,1,0:T(1,128)S(1)} %get-tuple-element.86), channel_id=1, source_target_pairs={{1,0},{2,1},{3,2},{5,4},{6,5},{7,6},{9,8},{10,9},{11,10},{13,12},{... | collective-permute-start | bytes 49160 | tf_op jit(solution)/shard_map/ppermute | solution.py:18
  35.2 7.1 %collective-permute-start.7 = (f32[4,1,1024]{2,1,0:T(1,128)S(1)}, f32[4,1,1024]{2,1,0:T(1,128)S(1)}, u32[]{:S(2)}, u32[]{:S(2)}) collective-permute-start(f32[4,1,1024]{2,1,0:T(1,128)S(1)} %get-tuple-element.81), channel_id=1, source_target_pairs={{0,1},{1,2},{2,3},{4,5},{5,6},{6,7},{8,9},{9,10},{10,11},{12,13},{... | collective-permute-start | bytes 49160 | tf_op jit(solution)/shard_map/ppermute | solution.py:15
  39.4 3.1 %collective-permute-start.6 = (f32[4,1,1024]{2,1,0:T(1,128)S(1)}, f32[4,1,1024]{2,1,0:T(1,128)S(1)}, u32[]{:S(2)}, u32[]{:S(2)}) collective-permute-start(f32[4,1,1024]{2,1,0:T(1,128)S(1)} %get-tuple-element.80), channel_id=1, source_target_pairs={{1,0},{2,1},{3,2},{5,4},{6,5},{7,6},{9,8},{10,9},{11,10},{13,12},{... | collective-permute-start | bytes 49160 | tf_op jit(solution)/shard_map/ppermute | solution.py:18
  42.8 7.1 %collective-permute-start.9 = (f32[4,1,1024]{2,1,0:T(1,128)S(1)}, f32[4,1,1024]{2,1,0:T(1,128)S(1)}, u32[]{:S(2)}, u32[]{:S(2)}) collective-permute-start(f32[4,1,1024]{2,1,0:T(1,128)S(1)} %get-tuple-element.75), channel_id=1, source_target_pairs={{0,1},{1,2},{2,3},{4,5},{5,6},{6,7},{8,9},{9,10},{10,11},{12,13},{... | collective-permute-start | bytes 49160 | tf_op jit(solution)/shard_map/ppermute | solution.py:15
  46.9 3.1 %collective-permute-start.8 = (f32[4,1,1024]{2,1,0:T(1,128)S(1)}, f32[4,1,1024]{2,1,0:T(1,128)S(1)}, u32[]{:S(2)}, u32[]{:S(2)}) collective-permute-start(f32[4,1,1024]{2,1,0:T(1,128)S(1)} %get-tuple-element.74), channel_id=1, source_target_pairs={{1,0},{2,1},{3,2},{5,4},{6,5},{7,6},{9,8},{10,9},{11,10},{13,12},{... | collective-permute-start | bytes 49160 | tf_op jit(solution)/shard_map/ppermute | solution.py:18
  50.4 7.1 %collective-permute-start.11 = (f32[4,1,1024]{2,1,0:T(1,128)S(1)}, f32[4,1,1024]{2,1,0:T(1,128)S(1)}, u32[]{:S(2)}, u32[]{:S(2)}) collective-permute-start(f32[4,1,1024]{2,1,0:T(1,128)S(1)} %get-tuple-element.69), channel_id=1, source_target_pairs={{0,1},{1,2},{2,3},{4,5},{5,6},{6,7},{8,9},{9,10},{10,11},{12,13},{... | collective-permute-start | bytes 49160 | tf_op jit(solution)/shard_map/ppermute | solution.py:15
  54.5 3.1 %collective-permute-start.10 = (f32[4,1,1024]{2,1,0:T(1,128)S(1)}, f32[4,1,1024]{2,1,0:T(1,128)S(1)}, u32[]{:S(2)}, u32[]{:S(2)}) collective-permute-start(f32[4,1,1024]{2,1,0:T(1,128)S(1)} %get-tuple-element.68), channel_id=1, source_target_pairs={{1,0},{2,1},{3,2},{5,4},{6,5},{7,6},{9,8},{10,9},{11,10},{13,12},{... | collective-permute-start | bytes 49160 | tf_op jit(solution)/shard_map/ppermute | solution.py:18
  57.9 7.3 %collective-permute-start.13 = (f32[4,1,1024]{2,1,0:T(1,128)S(1)}, f32[4,1,1024]{2,1,0:T(1,128)S(1)}, u32[]{:S(2)}, u32[]{:S(2)}) collective-permute-start(f32[4,1,1024]{2,1,0:T(1,128)S(1)} %get-tuple-element.63), channel_id=1, source_target_pairs={{0,1},{1,2},{2,3},{4,5},{5,6},{6,7},{8,9},{9,10},{10,11},{12,13},{... | collective-permute-start | bytes 49160 | tf_op jit(solution)/shard_map/ppermute | solution.py:15
  62.1 3.1 %collective-permute-start.12 = (f32[4,1,1024]{2,1,0:T(1,128)S(1)}, f32[4,1,1024]{2,1,0:T(1,128)S(1)}, u32[]{:S(2)}, u32[]{:S(2)}) collective-permute-start(f32[4,1,1024]{2,1,0:T(1,128)S(1)} %get-tuple-element.62), channel_id=1, source_target_pairs={{1,0},{2,1},{3,2},{5,4},{6,5},{7,6},{9,8},{10,9},{11,10},{13,12},{... | collective-permute-start | bytes 49160 | tf_op jit(solution)/shard_map/ppermute | solution.py:18
  65.5 16.1 %copy-start.4 = (f32[1,4]{1,0:T(1,128)S(1)}, f32[1,4]{1,0:T(1,128)}, u32[]{:S(2)}) copy-start(f32[1,4]{1,0:T(1,128)} %param.14) | copy-start | bytes 52
  65.6 5.5 %collective-permute-start.15 = (f32[4,1,1024]{2,1,0:T(1,128)S(1)}, f32[4,1,1024]{2,1,0:T(1,128)S(1)}, u32[]{:S(2)}, u32[]{:S(2)}) collective-permute-start(f32[4,1,1024]{2,1,0:T(1,128)S(1)} %get-tuple-element.57), channel_id=1, source_target_pairs={{0,1},{1,2},{2,3},{4,5},{5,6},{6,7},{8,9},{9,10},{10,11},{12,13},{... | collective-permute-start | bytes 49160 | tf_op jit(solution)/shard_map/ppermute | solution.py:15
  69.7 3.1 %collective-permute-start.14 = (f32[4,1,1024]{2,1,0:T(1,128)S(1)}, f32[4,1,1024]{2,1,0:T(1,128)S(1)}, u32[]{:S(2)}, u32[]{:S(2)}) collective-permute-start(f32[4,1,1024]{2,1,0:T(1,128)S(1)} %get-tuple-element.56), channel_id=1, source_target_pairs={{1,0},{2,1},{3,2},{5,4},{6,5},{7,6},{9,8},{10,9},{11,10},{13,12},{... | collective-permute-start | bytes 49160 | tf_op jit(solution)/shard_map/ppermute | solution.py:18
  73.0 8.6 %collective-permute-start.16 = (f32[4,16,1024]{2,1,0:T(8,128)S(1)}, f32[4,16,1024]{2,1,0:T(8,128)S(1)}, u32[]{:S(2)}, u32[]{:S(2)}) collective-permute-start(f32[4,16,1024]{2,1,0:T(8,128)S(1)} %fusion.33), channel_id=1, source_target_pairs={{0,4},{4,8},{8,12},{12,16},{16,20},{20,24},{24,28},{1,5},{5,9},{9,... | collective-permute-start | bytes 786440 | tf_op jit(solution)/shard_map/ppermute | solution.py:26
  81.7 10.9 %collective-permute-start.17 = (f32[4,16,1024]{2,1,0:T(8,128)S(1)}, f32[4,16,1024]{2,1,0:T(8,128)S(1)}, u32[]{:S(2)}, u32[]{:S(2)}) collective-permute-start(f32[4,16,1024]{2,1,0:T(8,128)S(1)} %subtract_multiply_fusion), channel_id=1, source_target_pairs={{4,0},{8,4},{12,8},{16,12},{20,16},{24,20},{28,24},{5,1},{9,5},{13... | collective-permute-start | bytes 786440 | tf_op jit(solution)/shard_map/ppermute | solution.py:26
  92.8 4.6 %collective-permute-start.21 = (f32[4,1,1024]{2,1,0:T(1,128)S(1)}, f32[4,1,1024]{2,1,0:T(1,128)S(1)}, u32[]{:S(2)}, u32[]{:S(2)}) collective-permute-start(f32[4,1,1024]{2,1,0:T(1,128)S(1)} %get-tuple-element.51), channel_id=1, source_target_pairs={{1,0},{2,1},{3,2},{5,4},{6,5},{7,6},{9,8},{10,9},{11,10},{13,12},{... | collective-permute-start | bytes 49160 | tf_op jit(solution)/shard_map/ppermute | solution.py:18
  94.1 3.9 %collective-permute-start.20 = (f32[4,1,1024]{2,1,0:T(1,128)S(1)}, f32[4,1,1024]{2,1,0:T(1,128)S(1)}, u32[]{:S(2)}, u32[]{:S(2)}) collective-permute-start(f32[4,1,1024]{2,1,0:T(1,128)S(1)} %get-tuple-element.50), channel_id=1, source_target_pairs={{0,1},{1,2},{2,3},{4,5},{5,6},{6,7},{8,9},{9,10},{10,11},{12,13},{... | collective-permute-start | bytes 49160 | tf_op jit(solution)/shard_map/ppermute | solution.py:15
  98.3 5.8 %collective-permute-start.23 = (f32[4,1,1024]{2,1,0:T(1,128)S(1)}, f32[4,1,1024]{2,1,0:T(1,128)S(1)}, u32[]{:S(2)}, u32[]{:S(2)}) collective-permute-start(f32[4,1,1024]{2,1,0:T(1,128)S(1)} %get-tuple-element.49), channel_id=1, source_target_pairs={{1,0},{2,1},{3,2},{5,4},{6,5},{7,6},{9,8},{10,9},{11,10},{13,12},{... | collective-permute-start | bytes 49160 | tf_op jit(solution)/shard_map/ppermute | solution.py:18
  99.6 5.0 %collective-permute-start.22 = (f32[4,1,1024]{2,1,0:T(1,128)S(1)}, f32[4,1,1024]{2,1,0:T(1,128)S(1)}, u32[]{:S(2)}, u32[]{:S(2)}) collective-permute-start(f32[4,1,1024]{2,1,0:T(1,128)S(1)} %get-tuple-element.48), channel_id=1, source_target_pairs={{0,1},{1,2},{2,3},{4,5},{5,6},{6,7},{8,9},{9,10},{10,11},{12,13},{... | collective-permute-start | bytes 49160 | tf_op jit(solution)/shard_map/ppermute | solution.py:15
  105.0 6.4 %collective-permute-start.25 = (f32[4,1,1024]{2,1,0:T(1,128)S(1)}, f32[4,1,1024]{2,1,0:T(1,128)S(1)}, u32[]{:S(2)}, u32[]{:S(2)}) collective-permute-start(f32[4,1,1024]{2,1,0:T(1,128)S(1)} %get-tuple-element.47), channel_id=1, source_target_pairs={{1,0},{2,1},{3,2},{5,4},{6,5},{7,6},{9,8},{10,9},{11,10},{13,12},{... | collective-permute-start | bytes 49160 | tf_op jit(solution)/shard_map/ppermute | solution.py:18
  106.3 5.7 %collective-permute-start.24 = (f32[4,1,1024]{2,1,0:T(1,128)S(1)}, f32[4,1,1024]{2,1,0:T(1,128)S(1)}, u32[]{:S(2)}, u32[]{:S(2)}) collective-permute-start(f32[4,1,1024]{2,1,0:T(1,128)S(1)} %get-tuple-element.46), channel_id=1, source_target_pairs={{0,1},{1,2},{2,3},{4,5},{5,6},{6,7},{8,9},{9,10},{10,11},{12,13},{... | collective-permute-start | bytes 49160 | tf_op jit(solution)/shard_map/ppermute | solution.py:15
  112.3 6.4 %collective-permute-start.27 = (f32[4,1,1024]{2,1,0:T(1,128)S(1)}, f32[4,1,1024]{2,1,0:T(1,128)S(1)}, u32[]{:S(2)}, u32[]{:S(2)}) collective-permute-start(f32[4,1,1024]{2,1,0:T(1,128)S(1)} %get-tuple-element.45), channel_id=1, source_target_pairs={{1,0},{2,1},{3,2},{5,4},{6,5},{7,6},{9,8},{10,9},{11,10},{13,12},{... | collective-permute-start | bytes 49160 | tf_op jit(solution)/shard_map/ppermute | solution.py:18
  113.6 5.7 %collective-permute-start.26 = (f32[4,1,1024]{2,1,0:T(1,128)S(1)}, f32[4,1,1024]{2,1,0:T(1,128)S(1)}, u32[]{:S(2)}, u32[]{:S(2)}) collective-permute-start(f32[4,1,1024]{2,1,0:T(1,128)S(1)} %get-tuple-element.44), channel_id=1, source_target_pairs={{0,1},{1,2},{2,3},{4,5},{5,6},{6,7},{8,9},{9,10},{10,11},{12,13},{... | collective-permute-start | bytes 49160 | tf_op jit(solution)/shard_map/ppermute | solution.py:15
  119.6 6.4 %collective-permute-start.29 = (f32[4,1,1024]{2,1,0:T(1,128)S(1)}, f32[4,1,1024]{2,1,0:T(1,128)S(1)}, u32[]{:S(2)}, u32[]{:S(2)}) collective-permute-start(f32[4,1,1024]{2,1,0:T(1,128)S(1)} %get-tuple-element.43), channel_id=1, source_target_pairs={{1,0},{2,1},{3,2},{5,4},{6,5},{7,6},{9,8},{10,9},{11,10},{13,12},{... | collective-permute-start | bytes 49160 | tf_op jit(solution)/shard_map/ppermute | solution.py:18
  120.9 5.7 %collective-permute-start.28 = (f32[4,1,1024]{2,1,0:T(1,128)S(1)}, f32[4,1,1024]{2,1,0:T(1,128)S(1)}, u32[]{:S(2)}, u32[]{:S(2)}) collective-permute-start(f32[4,1,1024]{2,1,0:T(1,128)S(1)} %get-tuple-element.42), channel_id=1, source_target_pairs={{0,1},{1,2},{2,3},{4,5},{5,6},{6,7},{8,9},{9,10},{10,11},{12,13},{... | collective-permute-start | bytes 49160 | tf_op jit(solution)/shard_map/ppermute | solution.py:15
  127.0 6.4 %collective-permute-start.31 = (f32[4,1,1024]{2,1,0:T(1,128)S(1)}, f32[4,1,1024]{2,1,0:T(1,128)S(1)}, u32[]{:S(2)}, u32[]{:S(2)}) collective-permute-start(f32[4,1,1024]{2,1,0:T(1,128)S(1)} %get-tuple-element.41), channel_id=1, source_target_pairs={{1,0},{2,1},{3,2},{5,4},{6,5},{7,6},{9,8},{10,9},{11,10},{13,12},{... | collective-permute-start | bytes 49160 | tf_op jit(solution)/shard_map/ppermute | solution.py:18
  128.3 5.7 %collective-permute-start.30 = (f32[4,1,1024]{2,1,0:T(1,128)S(1)}, f32[4,1,1024]{2,1,0:T(1,128)S(1)}, u32[]{:S(2)}, u32[]{:S(2)}) collective-permute-start(f32[4,1,1024]{2,1,0:T(1,128)S(1)} %get-tuple-element.40), channel_id=1, source_target_pairs={{0,1},{1,2},{2,3},{4,5},{5,6},{6,7},{8,9},{9,10},{10,11},{12,13},{... | collective-permute-start | bytes 49160 | tf_op jit(solution)/shard_map/ppermute | solution.py:15
  134.3 6.4 %collective-permute-start.33 = (f32[4,1,1024]{2,1,0:T(1,128)S(1)}, f32[4,1,1024]{2,1,0:T(1,128)S(1)}, u32[]{:S(2)}, u32[]{:S(2)}) collective-permute-start(f32[4,1,1024]{2,1,0:T(1,128)S(1)} %get-tuple-element.39), channel_id=1, source_target_pairs={{1,0},{2,1},{3,2},{5,4},{6,5},{7,6},{9,8},{10,9},{11,10},{13,12},{... | collective-permute-start | bytes 49160 | tf_op jit(solution)/shard_map/ppermute | solution.py:18
  135.6 5.7 %collective-permute-start.32 = (f32[4,1,1024]{2,1,0:T(1,128)S(1)}, f32[4,1,1024]{2,1,0:T(1,128)S(1)}, u32[]{:S(2)}, u32[]{:S(2)}) collective-permute-start(f32[4,1,1024]{2,1,0:T(1,128)S(1)} %get-tuple-element.38), channel_id=1, source_target_pairs={{0,1},{1,2},{2,3},{4,5},{5,6},{6,7},{8,9},{9,10},{10,11},{12,13},{... | collective-permute-start | bytes 49160 | tf_op jit(solution)/shard_map/ppermute | solution.py:15
  141.6 6.4 %collective-permute-start.35 = (f32[4,1,1024]{2,1,0:T(1,128)S(1)}, f32[4,1,1024]{2,1,0:T(1,128)S(1)}, u32[]{:S(2)}, u32[]{:S(2)}) collective-permute-start(f32[4,1,1024]{2,1,0:T(1,128)S(1)} %get-tuple-element.37), channel_id=1, source_target_pairs={{1,0},{2,1},{3,2},{5,4},{6,5},{7,6},{9,8},{10,9},{11,10},{13,12},{... | collective-permute-start | bytes 49160 | tf_op jit(solution)/shard_map/ppermute | solution.py:18
  142.9 5.7 %collective-permute-start.34 = (f32[4,1,1024]{2,1,0:T(1,128)S(1)}, f32[4,1,1024]{2,1,0:T(1,128)S(1)}, u32[]{:S(2)}, u32[]{:S(2)}) collective-permute-start(f32[4,1,1024]{2,1,0:T(1,128)S(1)} %get-tuple-element.36), channel_id=1, source_target_pairs={{0,1},{1,2},{2,3},{4,5},{5,6},{6,7},{8,9},{9,10},{10,11},{12,13},{... | collective-permute-start | bytes 49160 | tf_op jit(solution)/shard_map/ppermute | solution.py:15
  147.9 8.9 %copy-start.3 = (f32[8,4]{0,1:T(4,128)S(1)}, f32[8,4]{0,1:T(4,128)}, u32[]{:S(2)}) copy-start(f32[8,4]{0,1:T(4,128)} %param.15) | copy-start | bytes 388
  150.5 16.6 %all-to-all-start = ((f32[1,8,8192]{2,0,1:T(1,128)}), f32[1,8,8192]{2,0,1:T(1,128)S(1)}, u32[]{:S(2)}, u32[]{:S(2)}) async-start(f32[1,8,8192]{2,0,1:T(1,128)} %all_to_all.27), calls=%async_computation | async-start | bytes 524288 | tf_op jit(solution)/shard_map/all_to_all | solution.py:126
  185.9 50.6 %all-to-all-start.1 = ((f32[8,1,8192]{2,1,0:T(1,128)}), f32[8,1,8192]{2,1,0:T(1,128)S(1)}, u32[]{:S(2)}, u32[]{:S(2)}) async-start(f32[8,1,8192]{2,1,0:T(1,128)} %copy.67), calls=%async_computation.1 | async-start | bytes 524288 | tf_op jit(solution)/shard_map/all_to_all | solution.py:139
where the time goes:
time: 241 us; the launch traced here: 239 us
  starting transfers between devices  112 us (46%)
  blocking collectives  43.9 us (18%)
  local copies, waits for them, and re-layouts  37.5 us (16%)
  waiting for transfers between devices  18.6 us (8%)
  matrix products  13.5 us (6%)
  other arithmetic  8.53 us (4%)
  between operations  4.62 us (2%)
    ppermute x17, starting transfers between devices, padded_2(): lax.ppermute(lax.slice_in_dim(block, block.shape[dim] - width, None, axis...  73.3 us
    psum x1, blocking collectives, on_device(): square_sum = lax.psum(jnp.sum(gradient * gradient), ('tm', 'space'))  43.9 us
    ppermute x17, starting transfers between devices, padded_2(): lax.ppermute(lax.slice_in_dim(block, 0, width, axis=dim), axis, backward)  22.1 us
    slice x17, local copies, waits for them, and re-layouts, on_device(): lax.associative_scan(combine, (next_cols, inno_cols * forward_cols), reve...  16.4 us
    ppermute x2, waiting for transfers between devices, passed_along(): lax.ppermute(value, axis, [(source, source + steps) for source in range(l...  11.7 us
    dot_general x8, matrix products, select_rows(): jnp.einsum('kb,cbrx->kcrx', picker, blocks, precision=lax.Precision.HIGHEST)  7.44 us
    slice x11, local copies, waits for them, and re-layouts, on_device(): lax.associative_scan(combine, (rate_cols, inno_cols * columns), axis=0)[1]  7.18 us
    all_to_all x1, starting transfers between devices, on_device(): lax.all_to_all(flat_grad, 'tm', split_axis=1, concat_axis=0, tiled=True)  6.3 us
  transfers between devices with their start and end apart: 38, of which 16 were waited for; matrix products, arithmetic and copies ran while one was open for 13% of the time, Pallas kernels for 0%

commit v1 on v0

--- a/solution.py
+++ b/solution.py
@@ -123,7 +123,10 @@
     next_rates = jnp.concatenate([rates[1:], jnp.zeros((1, rates.shape[1]), jnp.float32)], axis=0)
     column_count = gradient.size // windows
     flat_grad = gradient.reshape(1, gradient.size)
-    columns = lax.all_to_all(flat_grad, "tm", split_axis=1, concat_axis=0, tiled=True)
+    columns = jnp.concatenate(
+        lax.all_to_all(jnp.stack(jnp.split(flat_grad, lax.axis_size("tm"), axis=1)), "tm", 0, 0),
+        axis=0,
+    )
     places = position * column_count + jnp.arange(column_count, dtype=jnp.int32)
     member = places // (field_shape[1] * field_shape[2])
     onehot = (member[None, :] == jnp.arange(field_shape[0], dtype=jnp.int32)[:, None]).astype(

time: 241 us -> 245 us (1.017)
  local copies, waits for them, and re-layouts: 37.5 us -> 41.7 us
    unnamed x10 -> x17, local copies, waits for them, and re-layouts: 0.03 us -> 4.35 us
where the time goes in v1:
time: 245 us; the launch traced here: 243 us
  starting transfers between devices  112 us (46%)
  blocking collectives  43.9 us (18%)
  local copies, waits for them, and re-layouts  41.7 us (17%)
  waiting for transfers between devices  18.6 us (8%)
  matrix products  13.5 us (6%)
  other arithmetic  8.53 us (3%)
  between operations  4.62 us (2%)
    ppermute x17, starting transfers between devices, padded_2(): lax.ppermute(lax.slice_in_dim(block, block.shape[dim] - width, None, axis...  73.3 us
    psum x1, blocking collectives, on_device(): square_sum = lax.psum(jnp.sum(gradient * gradient), ('tm', 'space'))  43.9 us
    ppermute x17, starting transfers between devices, padded_2(): lax.ppermute(lax.slice_in_dim(block, 0, width, axis=dim), axis, backward)  22.1 us
    slice x17, local copies, waits for them, and re-layouts, on_device(): lax.associative_scan(combine, (next_cols, inno_cols * forward_cols), reve...  16.4 us
    ppermute x2, waiting for transfers between devices, passed_along(): lax.ppermute(value, axis, [(source, source + steps) for source in range(l...  11.7 us
    dot_general x8, matrix products, select_rows(): jnp.einsum('kb,cbrx->kcrx', picker, blocks, precision=lax.Precision.HIGHEST)  7.44 us
    slice x11, local copies, waits for them, and re-layouts, on_device(): lax.associative_scan(combine, (rate_cols, inno_cols * columns), axis=0)[1]  7.18 us
    all_to_all x1, starting transfers between devices, on_device(): lax.all_to_all(jnp.stack(jnp.split(flat_grad, lax.axis_size('tm'), axis=1...  6.3 us
  transfers between devices with their start and end apart: 38, of which 16 were waited for; matrix products, arithmetic and copies ran while one was open for 13% of the time, Pallas kernels for 0%

profile of v1, /device:TPU:0, one launch (start us, length us, event | category | flops | bytes accessed | tf_op | source)
XLA Modules:
  0.0 243.3 jit_solution(3427168214540678982)
XLA Ops:
  1.6 2.4 collective-permute-start.1
  4.0 1.3 collective-permute-start
  7.0 1.3 collective-permute-start.19
  8.3 5.8 %collective-permute-start.18 = (f32[2,1,1024]{2,1,0:T(1,128)S(1)}, f32[2,1,1024]{2,1,0:T(1,128)S(1)}, u32[]{:S(2)}, u32[]{:S(2)}) collective-permute-start(f32[2,1,1024]{2,1,0:T(1,128)S(1)} %get-tuple-element.114), channel_id=1, source_target_pairs={{0,1},{1,2},{2,3},{4,5},{5,6},{6,7},{8,9},{9,10},{10,11},{12,13},{... | collective-permute-start | bytes 24584 | tf_op jit(solution)/shard_map/ppermute | solution.py:15
  17.1 1.7 fusion.169
  20.3 3.6 %collective-permute-start.3 = (f32[4,1,1024]{2,1,0:T(1,128)S(1)}, f32[4,1,1024]{2,1,0:T(1,128)S(1)}, u32[]{:S(2)}, u32[]{:S(2)}) collective-permute-start(f32[4,1,1024]{2,1,0:T(1,128)S(1)} %get-tuple-element.93), channel_id=1, source_target_pairs={{0,1},{1,2},{2,3},{4,5},{5,6},{6,7},{8,9},{9,10},{10,11},{12,13},{... | collective-permute-start | bytes 49160 | tf_op jit(solution)/shard_map/ppermute | solution.py:15
  24.0 1.3 collective-permute-start.2
  27.4 4.4 %collective-permute-start.5 = (f32[4,1,1024]{2,1,0:T(1,128)S(1)}, f32[4,1,1024]{2,1,0:T(1,128)S(1)}, u32[]{:S(2)}, u32[]{:S(2)}) collective-permute-start(f32[4,1,1024]{2,1,0:T(1,128)S(1)} %get-tuple-element.87), channel_id=1, source_target_pairs={{0,1},{1,2},{2,3},{4,5},{5,6},{6,7},{8,9},{9,10},{10,11},{12,13},{... | collective-permute-start | bytes 49160 | tf_op jit(solution)/shard_map/ppermute | solution.py:15
  31.8 1.3 collective-permute-start.4
  35.2 4.2 %collective-permute-start.7 = (f32[4,1,1024]{2,1,0:T(1,128)S(1)}, f32[4,1,1024]{2,1,0:T(1,128)S(1)}, u32[]{:S(2)}, u32[]{:S(2)}) collective-permute-start(f32[4,1,1024]{2,1,0:T(1,128)S(1)} %get-tuple-element.81), channel_id=1, source_target_pairs={{0,1},{1,2},{2,3},{4,5},{5,6},{6,7},{8,9},{9,10},{10,11},{12,13},{... | collective-permute-start | bytes 49160 | tf_op jit(solution)/shard_map/ppermute | solution.py:15
  39.4 1.3 collective-permute-start.6
  42.8 4.2 %collective-permute-start.9 = (f32[4,1,1024]{2,1,0:T(1,128)S(1)}, f32[4,1,1024]{2,1,0:T(1,128)S(1)}, u32[]{:S(2)}, u32[]{:S(2)}) collective-permute-start(f32[4,1,1024]{2,1,0:T(1,128)S(1)} %get-tuple-element.75), channel_id=1, source_target_pairs={{0,1},{1,2},{2,3},{4,5},{5,6},{6,7},{8,9},{9,10},{10,11},{12,13},{... | collective-permute-start | bytes 49160 | tf_op jit(solution)/shard_map/ppermute | solution.py:15
  46.9 1.3 collective-permute-start.8
  50.4 4.2 %collective-permute-start.11 = (f32[4,1,1024]{2,1,0:T(1,128)S(1)}, f32[4,1,1024]{2,1,0:T(1,128)S(1)}, u32[]{:S(2)}, u32[]{:S(2)}) collective-permute-start(f32[4,1,1024]{2,1,0:T(1,128)S(1)} %get-tuple-element.69), channel_id=1, source_target_pairs={{0,1},{1,2},{2,3},{4,5},{5,6},{6,7},{8,9},{9,10},{10,11},{12,13},{... | collective-permute-start | bytes 49160 | tf_op jit(solution)/shard_map/ppermute | solution.py:15
  54.5 1.3 collective-permute-start.10
  57.9 4.2 %collective-permute-start.13 = (f32[4,1,1024]{2,1,0:T(1,128)S(1)}, f32[4,1,1024]{2,1,0:T(1,128)S(1)}, u32[]{:S(2)}, u32[]{:S(2)}) collective-permute-start(f32[4,1,1024]{2,1,0:T(1,128)S(1)} %get-tuple-element.63), channel_id=1, source_target_pairs={{0,1},{1,2},{2,3},{4,5},{5,6},{6,7},{8,9},{9,10},{10,11},{12,13},{... | collective-permute-start | bytes 49160 | tf_op jit(solution)/shard_map/ppermute | solution.py:15
  62.1 1.5 collective-permute-start.12
  65.6 4.1 %collective-permute-start.15 = (f32[4,1,1024]{2,1,0:T(1,128)S(1)}, f32[4,1,1024]{2,1,0:T(1,128)S(1)}, u32[]{:S(2)}, u32[]{:S(2)}) collective-permute-start(f32[4,1,1024]{2,1,0:T(1,128)S(1)} %get-tuple-element.57), channel_id=1, source_target_pairs={{0,1},{1,2},{2,3},{4,5},{5,6},{6,7},{8,9},{9,10},{10,11},{12,13},{... | collective-permute-start | bytes 49160 | tf_op jit(solution)/shard_map/ppermute | solution.py:15
  69.7 1.3 collective-permute-start.14
  71.1 1.7 collective-permute-done.14
  73.0 3.4 %collective-permute-start.16 = (f32[4,16,1024]{2,1,0:T(8,128)S(1)}, f32[4,16,1024]{2,1,0:T(8,128)S(1)}, u32[]{:S(2)}, u32[]{:S(2)}) collective-permute-start(f32[4,16,1024]{2,1,0:T(8,128)S(1)} %fusion.33), channel_id=1, source_target_pairs={{0,4},{4,8},{8,12},{12,16},{16,20},{20,24},{24,28},{1,5},{5,9},{9,... | collective-permute-start | bytes 786440 | tf_op jit(solution)/shard_map/ppermute | solution.py:26
  78.0 3.6 %collective-permute-done.16 = f32[4,16,1024]{2,1,0:T(8,128)S(1)} collective-permute-done((f32[4,16,1024]{2,1,0:T(8,128)S(1)}, f32[4,16,1024]{2,1,0:T(8,128)S(1)}, u32[]{:S(2)}, u32[]{:S(2)}) %collective-permute-start.16) | collective-permute-done | bytes 262176 | tf_op jit(solution)/shard_map/ppermute | solution.py:26
  81.7 1.3 collective-permute-start.17
  84.6 8.1 %collective-permute-done.17 = f32[4,16,1024]{2,1,0:T(8,128)S(1)} collective-permute-done((f32[4,16,1024]{2,1,0:T(8,128)S(1)}, f32[4,16,1024]{2,1,0:T(8,128)S(1)}, u32[]{:S(2)}, u32[]{:S(2)}) %collective-permute-start.17) | collective-permute-done | bytes 262176 | tf_op jit(solution)/shard_map/ppermute | solution.py:26
  92.8 1.3 collective-permute-start.21
  94.1 3.0 %collective-permute-start.20 = (f32[4,1,1024]{2,1,0:T(1,128)S(1)}, f32[4,1,1024]{2,1,0:T(1,128)S(1)}, u32[]{:S(2)}, u32[]{:S(2)}) collective-permute-start(f32[4,1,1024]{2,1,0:T(1,128)S(1)} %get-tuple-element.50), channel_id=1, source_target_pairs={{0,1},{1,2},{2,3},{4,5},{5,6},{6,7},{8,9},{9,10},{10,11},{12,13},{... | collective-permute-start | bytes 49160 | tf_op jit(solution)/shard_map/ppermute | solution.py:15
  98.3 1.3 collective-permute-start.23
  99.6 4.2 %collective-permute-start.22 = (f32[4,1,1024]{2,1,0:T(1,128)S(1)}, f32[4,1,1024]{2,1,0:T(1,128)S(1)}, u32[]{:S(2)}, u32[]{:S(2)}) collective-permute-start(f32[4,1,1024]{2,1,0:T(1,128)S(1)} %get-tuple-element.48), channel_id=1, source_target_pairs={{0,1},{1,2},{2,3},{4,5},{5,6},{6,7},{8,9},{9,10},{10,11},{12,13},{... | collective-permute-start | bytes 49160 | tf_op jit(solution)/shard_map/ppermute | solution.py:15
  105.0 1.3 collective-permute-start.25
  106.3 4.9 %collective-permute-start.24 = (f32[4,1,1024]{2,1,0:T(1,128)S(1)}, f32[4,1,1024]{2,1,0:T(1,128)S(1)}, u32[]{:S(2)}, u32[]{:S(2)}) collective-permute-start(f32[4,1,1024]{2,1,0:T(1,128)S(1)} %get-tuple-element.46), channel_id=1, source_target_pairs={{0,1},{1,2},{2,3},{4,5},{5,6},{6,7},{8,9},{9,10},{10,11},{12,13},{... | collective-permute-start | bytes 49160 | tf_op jit(solution)/shard_map/ppermute | solution.py:15
  112.3 1.3 collective-permute-start.27
  113.6 4.9 %collective-permute-start.26 = (f32[4,1,1024]{2,1,0:T(1,128)S(1)}, f32[4,1,1024]{2,1,0:T(1,128)S(1)}, u32[]{:S(2)}, u32[]{:S(2)}) collective-permute-start(f32[4,1,1024]{2,1,0:T(1,128)S(1)} %get-tuple-element.44), channel_id=1, source_target_pairs={{0,1},{1,2},{2,3},{4,5},{5,6},{6,7},{8,9},{9,10},{10,11},{12,13},{... | collective-permute-start | bytes 49160 | tf_op jit(solution)/shard_map/ppermute | solution.py:15
  119.6 1.3 collective-permute-start.29
  120.9 4.9 %collective-permute-start.28 = (f32[4,1,1024]{2,1,0:T(1,128)S(1)}, f32[4,1,1024]{2,1,0:T(1,128)S(1)}, u32[]{:S(2)}, u32[]{:S(2)}) collective-permute-start(f32[4,1,1024]{2,1,0:T(1,128)S(1)} %get-tuple-element.42), channel_id=1, source_target_pairs={{0,1},{1,2},{2,3},{4,5},{5,6},{6,7},{8,9},{9,10},{10,11},{12,13},{... | collective-permute-start | bytes 49160 | tf_op jit(solution)/shard_map/ppermute | solution.py:15
  127.0 1.3 collective-permute-start.31
  128.3 4.9 %collective-permute-start.30 = (f32[4,1,1024]{2,1,0:T(1,128)S(1)}, f32[4,1,1024]{2,1,0:T(1,128)S(1)}, u32[]{:S(2)}, u32[]{:S(2)}) collective-permute-start(f32[4,1,1024]{2,1,0:T(1,128)S(1)} %get-tuple-element.40), channel_id=1, source_target_pairs={{0,1},{1,2},{2,3},{4,5},{5,6},{6,7},{8,9},{9,10},{10,11},{12,13},{... | collective-permute-start | bytes 49160 | tf_op jit(solution)/shard_map/ppermute | solution.py:15
  134.3 1.3 collective-permute-start.33
  135.6 4.9 %collective-permute-start.32 = (f32[4,1,1024]{2,1,0:T(1,128)S(1)}, f32[4,1,1024]{2,1,0:T(1,128)S(1)}, u32[]{:S(2)}, u32[]{:S(2)}) collective-permute-start(f32[4,1,1024]{2,1,0:T(1,128)S(1)} %get-tuple-element.38), channel_id=1, source_target_pairs={{0,1},{1,2},{2,3},{4,5},{5,6},{6,7},{8,9},{9,10},{10,11},{12,13},{... | collective-permute-start | bytes 49160 | tf_op jit(solution)/shard_map/ppermute | solution.py:15
  142.9 4.9 %collective-permute-start.34 = (f32[4,1,1024]{2,1,0:T(1,128)S(1)}, f32[4,1,1024]{2,1,0:T(1,128)S(1)}, u32[]{:S(2)}, u32[]{:S(2)}) collective-permute-start(f32[4,1,1024]{2,1,0:T(1,128)S(1)} %get-tuple-element.36), channel_id=1, source_target_pairs={{0,1},{1,2},{2,3},{4,5},{5,6},{6,7},{8,9},{9,10},{10,11},{12,13},{... | collective-permute-start | bytes 49160 | tf_op jit(solution)/shard_map/ppermute | solution.py:15
  154.7 6.3 %all-to-all-start = ((f32[8,1,8192]{2,1,0:T(1,128)}), f32[8,1,8192]{2,1,0:T(1,128)S(1)}, u32[]{:S(2)}, u32[]{:S(2)}) async-start(f32[8,1,8192]{2,1,0:T(1,128)} %fusion.112), calls=%async_computation | async-start | bytes 524288 | tf_op jit(solution)/shard_map/all_to_all | solution.py:127
  166.6 1.6 slice.797
  168.2 1.6 slice.806
  169.8 1.6 slice.799
  180.1 1.6 slice.803
  181.6 1.6 slice.801
  185.9 1.6 slice.819
  190.1 6.0 %all-to-all-start.1 = ((f32[8,1,8192]{2,1,0:T(1,128)}), f32[8,1,8192]{2,1,0:T(1,128)S(1)}, u32[]{:S(2)}, u32[]{:S(2)}) async-start(f32[8,1,8192]{2,1,0:T(1,128)} %copy.66), calls=%async_computation.1 | async-start | bytes 524288 | tf_op jit(solution)/shard_map/all_to_all | solution.py:142
  196.1 43.9 %psum.7 = f32[]{:T(128)} all-reduce(f32[]{:T(128)} %get-tuple-element.10), channel_id=1, replica_groups=mesh['tm'=8,'space'=4] {'tm','space'}, use_global_device_ids=true, to_apply=%region_1.2 | all-reduce | flops 1 | bytes 8 | tf_op jit(solution)/shard_map/psum | solution.py:117
  (228 shorter events, 59.2 us)
Async XLA Ops:
  1.6 18.3 %collective-permute-start.1 = (f32[4,1,1024]{2,1,0:T(1,128)S(1)}, f32[4,1,1024]{2,1,0:T(1,128)S(1)}, u32[]{:S(2)}, u32[]{:S(2)}) collective-permute-start(f32[4,1,1024]{2,1,0:T(1,128)S(1)} %get-tuple-element.99), channel_id=1, source_target_pairs={{0,1},{1,2},{2,3},{4,5},{5,6},{6,7},{8,9},{9,10},{10,11},{12,13},{... | collective-permute-start | bytes 49160 | tf_op jit(solution)/shard_map/ppermute | solution.py:15
  4.0 15.9 %collective-permute-start = (f32[4,1,1024]{2,1,0:T(1,128)S(1)}, f32[4,1,1024]{2,1,0:T(1,128)S(1)}, u32[]{:S(2)}, u32[]{:S(2)}) collective-permute-start(f32[4,1,1024]{2,1,0:T(1,128)S(1)} %get-tuple-element.98), channel_id=1, source_target_pairs={{1,0},{2,1},{3,2},{5,4},{6,5},{7,6},{9,8},{10,9},{11,10},{13,12},{... | collective-permute-start | bytes 49160 | tf_op jit(solution)/shard_map/ppermute | solution.py:18
  7.0 12.8 %collective-permute-start.19 = (f32[2,1,1024]{2,1,0:T(1,128)S(1)}, f32[2,1,1024]{2,1,0:T(1,128)S(1)}, u32[]{:S(2)}, u32[]{:S(2)}) collective-permute-start(f32[2,1,1024]{2,1,0:T(1,128)S(1)} %get-tuple-element.115), channel_id=1, source_target_pairs={{1,0},{2,1},{3,2},{5,4},{6,5},{7,6},{9,8},{10,9},{11,10},{13,12},{... | collective-permute-start | bytes 24584 | tf_op jit(solution)/shard_map/ppermute | solution.py:18
  8.3 11.5 %collective-permute-start.18 = (f32[2,1,1024]{2,1,0:T(1,128)S(1)}, f32[2,1,1024]{2,1,0:T(1,128)S(1)}, u32[]{:S(2)}, u32[]{:S(2)}) collective-permute-start(f32[2,1,1024]{2,1,0:T(1,128)S(1)} %get-tuple-element.114), channel_id=1, source_target_pairs={{0,1},{1,2},{2,3},{4,5},{5,6},{6,7},{8,9},{9,10},{10,11},{12,13},{... | collective-permute-start | bytes 24584 | tf_op jit(solution)/shard_map/ppermute | solution.py:15
  17.1 1.8 copy-start.2
  17.1 2.7 %copy-start.1 = (f32[1,16,1024]{2,1,0:T(8,128)S(1)}, f32[1,16,1024]{2,1,0:T(8,128)}, u32[]{:S(2)}) copy-start(f32[1,16,1024]{2,1,0:T(8,128)} %param.10) | copy-start | bytes 196612
  17.1 2.9 %copy-start = (f32[1,4,16,1024]{3,2,1,0:T(8,128)S(1)}, f32[1,4,16,1024]{3,2,1,0:T(8,128)}, u32[]{:S(2)}) copy-start(f32[1,4,16,1024]{3,2,1,0:T(8,128)} %param.8) | copy-start | bytes 786436
  20.3 6.6 %collective-permute-start.3 = (f32[4,1,1024]{2,1,0:T(1,128)S(1)}, f32[4,1,1024]{2,1,0:T(1,128)S(1)}, u32[]{:S(2)}, u32[]{:S(2)}) collective-permute-start(f32[4,1,1024]{2,1,0:T(1,128)S(1)} %get-tuple-element.93), channel_id=1, source_target_pairs={{0,1},{1,2},{2,3},{4,5},{5,6},{6,7},{8,9},{9,10},{10,11},{12,13},{... | collective-permute-start | bytes 49160 | tf_op jit(solution)/shard_map/ppermute | solution.py:15
  24.0 3.1 %collective-permute-start.2 = (f32[4,1,1024]{2,1,0:T(1,128)S(1)}, f32[4,1,1024]{2,1,0:T(1,128)S(1)}, u32[]{:S(2)}, u32[]{:S(2)}) collective-permute-start(f32[4,1,1024]{2,1,0:T(1,128)S(1)} %get-tuple-element.92), channel_id=1, source_target_pairs={{1,0},{2,1},{3,2},{5,4},{6,5},{7,6},{9,8},{10,9},{11,10},{13,12},{... | collective-permute-start | bytes 49160 | tf_op jit(solution)/shard_map/ppermute | solution.py:18
  27.4 7.3 %collective-permute-start.5 = (f32[4,1,1024]{2,1,0:T(1,128)S(1)}, f32[4,1,1024]{2,1,0:T(1,128)S(1)}, u32[]{:S(2)}, u32[]{:S(2)}) collective-permute-start(f32[4,1,1024]{2,1,0:T(1,128)S(1)} %get-tuple-element.87), channel_id=1, source_target_pairs={{0,1},{1,2},{2,3},{4,5},{5,6},{6,7},{8,9},{9,10},{10,11},{12,13},{... | collective-permute-start | bytes 49160 | tf_op jit(solution)/shard_map/ppermute | solution.py:15
  31.8 3.1 %collective-permute-start.4 = (f32[4,1,1024]{2,1,0:T(1,128)S(1)}, f32[4,1,1024]{2,1,0:T(1,128)S(1)}, u32[]{:S(2)}, u32[]{:S(2)}) collective-permute-start(f32[4,1,1024]{2,1,0:T(1,128)S(1)} %get-tuple-element.86), channel_id=1, source_target_pairs={{1,0},{2,1},{3,2},{5,4},{6,5},{7,6},{9,8},{10,9},{11,10},{13,12},{... | collective-permute-start | bytes 49160 | tf_op jit(solution)/shard_map/ppermute | solution.py:18
  35.2 7.1 %collective-permute-start.7 = (f32[4,1,1024]{2,1,0:T(1,128)S(1)}, f32[4,1,1024]{2,1,0:T(1,128)S(1)}, u32[]{:S(2)}, u32[]{:S(2)}) collective-permute-start(f32[4,1,1024]{2,1,0:T(1,128)S(1)} %get-tuple-element.81), channel_id=1, source_target_pairs={{0,1},{1,2},{2,3},{4,5},{5,6},{6,7},{8,9},{9,10},{10,11},{12,13},{... | collective-permute-start | bytes 49160 | tf_op jit(solution)/shard_map/ppermute | solution.py:15
  39.4 3.1 %collective-permute-start.6 = (f32[4,1,1024]{2,1,0:T(1,128)S(1)}, f32[4,1,1024]{2,1,0:T(1,128)S(1)}, u32[]{:S(2)}, u32[]{:S(2)}) collective-permute-start(f32[4,1,1024]{2,1,0:T(1,128)S(1)} %get-tuple-element.80), channel_id=1, source_target_pairs={{1,0},{2,1},{3,2},{5,4},{6,5},{7,6},{9,8},{10,9},{11,10},{13,12},{... | collective-permute-start | bytes 49160 | tf_op jit(solution)/shard_map/ppermute | solution.py:18
  42.8 7.1 %collective-permute-start.9 = (f32[4,1,1024]{2,1,0:T(1,128)S(1)}, f32[4,1,1024]{2,1,0:T(1,128)S(1)}, u32[]{:S(2)}, u32[]{:S(2)}) collective-permute-start(f32[4,1,1024]{2,1,0:T(1,128)S(1)} %get-tuple-element.75), channel_id=1, source_target_pairs={{0,1},{1,2},{2,3},{4,5},{5,6},{6,7},{8,9},{9,10},{10,11},{12,13},{... | collective-permute-start | bytes 49160 | tf_op jit(solution)/shard_map/ppermute | solution.py:15
  46.9 3.1 %collective-permute-start.8 = (f32[4,1,1024]{2,1,0:T(1,128)S(1)}, f32[4,1,1024]{2,1,0:T(1,128)S(1)}, u32[]{:S(2)}, u32[]{:S(2)}) collective-permute-start(f32[4,1,1024]{2,1,0:T(1,128)S(1)} %get-tuple-element.74), channel_id=1, source_target_pairs={{1,0},{2,1},{3,2},{5,4},{6,5},{7,6},{9,8},{10,9},{11,10},{13,12},{... | collective-permute-start | bytes 49160 | tf_op jit(solution)/shard_map/ppermute | solution.py:18
  50.4 7.1 %collective-permute-start.11 = (f32[4,1,1024]{2,1,0:T(1,128)S(1)}, f32[4,1,1024]{2,1,0:T(1,128)S(1)}, u32[]{:S(2)}, u32[]{:S(2)}) collective-permute-start(f32[4,1,1024]{2,1,0:T(1,128)S(1)} %get-tuple-element.69), channel_id=1, source_target_pairs={{0,1},{1,2},{2,3},{4,5},{5,6},{6,7},{8,9},{9,10},{10,11},{12,13},{... | collective-permute-start | bytes 49160 | tf_op jit(solution)/shard_map/ppermute | solution.py:15
  54.5 3.1 %collective-permute-start.10 = (f32[4,1,1024]{2,1,0:T(1,128)S(1)}, f32[4,1,1024]{2,1,0:T(1,128)S(1)}, u32[]{:S(2)}, u32[]{:S(2)}) collective-permute-start(f32[4,1,1024]{2,1,0:T(1,128)S(1)} %get-tuple-element.68), channel_id=1, source_target_pairs={{1,0},{2,1},{3,2},{5,4},{6,5},{7,6},{9,8},{10,9},{11,10},{13,12},{... | collective-permute-start | bytes 49160 | tf_op jit(solution)/shard_map/ppermute | solution.py:18
  57.9 7.3 %collective-permute-start.13 = (f32[4,1,1024]{2,1,0:T(1,128)S(1)}, f32[4,1,1024]{2,1,0:T(1,128)S(1)}, u32[]{:S(2)}, u32[]{:S(2)}) collective-permute-start(f32[4,1,1024]{2,1,0:T(1,128)S(1)} %get-tuple-element.63), channel_id=1, source_target_pairs={{0,1},{1,2},{2,3},{4,5},{5,6},{6,7},{8,9},{9,10},{10,11},{12,13},{... | collective-permute-start | bytes 49160 | tf_op jit(solution)/shard_map/ppermute | solution.py:15
  62.1 3.1 %collective-permute-start.12 = (f32[4,1,1024]{2,1,0:T(1,128)S(1)}, f32[4,1,1024]{2,1,0:T(1,128)S(1)}, u32[]{:S(2)}, u32[]{:S(2)}) collective-permute-start(f32[4,1,1024]{2,1,0:T(1,128)S(1)} %get-tuple-element.62), channel_id=1, source_target_pairs={{1,0},{2,1},{3,2},{5,4},{6,5},{7,6},{9,8},{10,9},{11,10},{13,12},{... | collective-permute-start | bytes 49160 | tf_op jit(solution)/shard_map/ppermute | solution.py:18
  65.5 16.1 %copy-start.4 = (f32[1,4]{1,0:T(1,128)S(1)}, f32[1,4]{1,0:T(1,128)}, u32[]{:S(2)}) copy-start(f32[1,4]{1,0:T(1,128)} %param.14) | copy-start | bytes 52
  65.6 5.5 %collective-permute-start.15 = (f32[4,1,1024]{2,1,0:T(1,128)S(1)}, f32[4,1,1024]{2,1,0:T(1,128)S(1)}, u32[]{:S(2)}, u32[]{:S(2)}) collective-permute-start(f32[4,1,1024]{2,1,0:T(1,128)S(1)} %get-tuple-element.57), channel_id=1, source_target_pairs={{0,1},{1,2},{2,3},{4,5},{5,6},{6,7},{8,9},{9,10},{10,11},{12,13},{... | collective-permute-start | bytes 49160 | tf_op jit(solution)/shard_map/ppermute | solution.py:15
  69.7 3.1 %collective-permute-start.14 = (f32[4,1,1024]{2,1,0:T(1,128)S(1)}, f32[4,1,1024]{2,1,0:T(1,128)S(1)}, u32[]{:S(2)}, u32[]{:S(2)}) collective-permute-start(f32[4,1,1024]{2,1,0:T(1,128)S(1)} %get-tuple-element.56), channel_id=1, source_target_pairs={{1,0},{2,1},{3,2},{5,4},{6,5},{7,6},{9,8},{10,9},{11,10},{13,12},{... | collective-permute-start | bytes 49160 | tf_op jit(solution)/shard_map/ppermute | solution.py:18
  73.0 8.6 %collective-permute-start.16 = (f32[4,16,1024]{2,1,0:T(8,128)S(1)}, f32[4,16,1024]{2,1,0:T(8,128)S(1)}, u32[]{:S(2)}, u32[]{:S(2)}) collective-permute-start(f32[4,16,1024]{2,1,0:T(8,128)S(1)} %fusion.33), channel_id=1, source_target_pairs={{0,4},{4,8},{8,12},{12,16},{16,20},{20,24},{24,28},{1,5},{5,9},{9,... | collective-permute-start | bytes 786440 | tf_op jit(solution)/shard_map/ppermute | solution.py:26
  81.7 10.9 %collective-permute-start.17 = (f32[4,16,1024]{2,1,0:T(8,128)S(1)}, f32[4,16,1024]{2,1,0:T(8,128)S(1)}, u32[]{:S(2)}, u32[]{:S(2)}) collective-permute-start(f32[4,16,1024]{2,1,0:T(8,128)S(1)} %subtract_multiply_fusion), channel_id=1, source_target_pairs={{4,0},{8,4},{12,8},{16,12},{20,16},{24,20},{28,24},{5,1},{9,5},{13... | collective-permute-start | bytes 786440 | tf_op jit(solution)/shard_map/ppermute | solution.py:26
  92.8 4.6 %collective-permute-start.21 = (f32[4,1,1024]{2,1,0:T(1,128)S(1)}, f32[4,1,1024]{2,1,0:T(1,128)S(1)}, u32[]{:S(2)}, u32[]{:S(2)}) collective-permute-start(f32[4,1,1024]{2,1,0:T(1,128)S(1)} %get-tuple-element.51), channel_id=1, source_target_pairs={{1,0},{2,1},{3,2},{5,4},{6,5},{7,6},{9,8},{10,9},{11,10},{13,12},{... | collective-permute-start | bytes 49160 | tf_op jit(solution)/shard_map/ppermute | solution.py:18
  94.1 3.9 %collective-permute-start.20 = (f32[4,1,1024]{2,1,0:T(1,128)S(1)}, f32[4,1,1024]{2,1,0:T(1,128)S(1)}, u32[]{:S(2)}, u32[]{:S(2)}) collective-permute-start(f32[4,1,1024]{2,1,0:T(1,128)S(1)} %get-tuple-element.50), channel_id=1, source_target_pairs={{0,1},{1,2},{2,3},{4,5},{5,6},{6,7},{8,9},{9,10},{10,11},{12,13},{... | collective-permute-start | bytes 49160 | tf_op jit(solution)/shard_map/ppermute | solution.py:15
  98.3 5.8 %collective-permute-start.23 = (f32[4,1,1024]{2,1,0:T(1,128)S(1)}, f32[4,1,1024]{2,1,0:T(1,128)S(1)}, u32[]{:S(2)}, u32[]{:S(2)}) collective-permute-start(f32[4,1,1024]{2,1,0:T(1,128)S(1)} %get-tuple-element.49), channel_id=1, source_target_pairs={{1,0},{2,1},{3,2},{5,4},{6,5},{7,6},{9,8},{10,9},{11,10},{13,12},{... | collective-permute-start | bytes 49160 | tf_op jit(solution)/shard_map/ppermute | solution.py:18
  99.6 5.0 %collective-permute-start.22 = (f32[4,1,1024]{2,1,0:T(1,128)S(1)}, f32[4,1,1024]{2,1,0:T(1,128)S(1)}, u32[]{:S(2)}, u32[]{:S(2)}) collective-permute-start(f32[4,1,1024]{2,1,0:T(1,128)S(1)} %get-tuple-element.48), channel_id=1, source_target_pairs={{0,1},{1,2},{2,3},{4,5},{5,6},{6,7},{8,9},{9,10},{10,11},{12,13},{... | collective-permute-start | bytes 49160 | tf_op jit(solution)/shard_map/ppermute | solution.py:15
  105.0 6.4 %collective-permute-start.25 = (f32[4,1,1024]{2,1,0:T(1,128)S(1)}, f32[4,1,1024]{2,1,0:T(1,128)S(1)}, u32[]{:S(2)}, u32[]{:S(2)}) collective-permute-start(f32[4,1,1024]{2,1,0:T(1,128)S(1)} %get-tuple-element.47), channel_id=1, source_target_pairs={{1,0},{2,1},{3,2},{5,4},{6,5},{7,6},{9,8},{10,9},{11,10},{13,12},{... | collective-permute-start | bytes 49160 | tf_op jit(solution)/shard_map/ppermute | solution.py:18
  106.3 5.7 %collective-permute-start.24 = (f32[4,1,1024]{2,1,0:T(1,128)S(1)}, f32[4,1,1024]{2,1,0:T(1,128)S(1)}, u32[]{:S(2)}, u32[]{:S(2)}) collective-permute-start(f32[4,1,1024]{2,1,0:T(1,128)S(1)} %get-tuple-element.46), channel_id=1, source_target_pairs={{0,1},{1,2},{2,3},{4,5},{5,6},{6,7},{8,9},{9,10},{10,11},{12,13},{... | collective-permute-start | bytes 49160 | tf_op jit(solution)/shard_map/ppermute | solution.py:15
  112.3 6.4 %collective-permute-start.27 = (f32[4,1,1024]{2,1,0:T(1,128)S(1)}, f32[4,1,1024]{2,1,0:T(1,128)S(1)}, u32[]{:S(2)}, u32[]{:S(2)}) collective-permute-start(f32[4,1,1024]{2,1,0:T(1,128)S(1)} %get-tuple-element.45), channel_id=1, source_target_pairs={{1,0},{2,1},{3,2},{5,4},{6,5},{7,6},{9,8},{10,9},{11,10},{13,12},{... | collective-permute-start | bytes 49160 | tf_op jit(solution)/shard_map/ppermute | solution.py:18
  113.6 5.7 %collective-permute-start.26 = (f32[4,1,1024]{2,1,0:T(1,128)S(1)}, f32[4,1,1024]{2,1,0:T(1,128)S(1)}, u32[]{:S(2)}, u32[]{:S(2)}) collective-permute-start(f32[4,1,1024]{2,1,0:T(1,128)S(1)} %get-tuple-element.44), channel_id=1, source_target_pairs={{0,1},{1,2},{2,3},{4,5},{5,6},{6,7},{8,9},{9,10},{10,11},{12,13},{... | collective-permute-start | bytes 49160 | tf_op jit(solution)/shard_map/ppermute | solution.py:15
  119.6 6.4 %collective-permute-start.29 = (f32[4,1,1024]{2,1,0:T(1,128)S(1)}, f32[4,1,1024]{2,1,0:T(1,128)S(1)}, u32[]{:S(2)}, u32[]{:S(2)}) collective-permute-start(f32[4,1,1024]{2,1,0:T(1,128)S(1)} %get-tuple-element.43), channel_id=1, source_target_pairs={{1,0},{2,1},{3,2},{5,4},{6,5},{7,6},{9,8},{10,9},{11,10},{13,12},{... | collective-permute-start | bytes 49160 | tf_op jit(solution)/shard_map/ppermute | solution.py:18
  120.9 5.7 %collective-permute-start.28 = (f32[4,1,1024]{2,1,0:T(1,128)S(1)}, f32[4,1,1024]{2,1,0:T(1,128)S(1)}, u32[]{:S(2)}, u32[]{:S(2)}) collective-permute-start(f32[4,1,1024]{2,1,0:T(1,128)S(1)} %get-tuple-element.42), channel_id=1, source_target_pairs={{0,1},{1,2},{2,3},{4,5},{5,6},{6,7},{8,9},{9,10},{10,11},{12,13},{... | collective-permute-start | bytes 49160 | tf_op jit(solution)/shard_map/ppermute | solution.py:15
  127.0 6.4 %collective-permute-start.31 = (f32[4,1,1024]{2,1,0:T(1,128)S(1)}, f32[4,1,1024]{2,1,0:T(1,128)S(1)}, u32[]{:S(2)}, u32[]{:S(2)}) collective-permute-start(f32[4,1,1024]{2,1,0:T(1,128)S(1)} %get-tuple-element.41), channel_id=1, source_target_pairs={{1,0},{2,1},{3,2},{5,4},{6,5},{7,6},{9,8},{10,9},{11,10},{13,12},{... | collective-permute-start | bytes 49160 | tf_op jit(solution)/shard_map/ppermute | solution.py:18
  128.3 5.7 %collective-permute-start.30 = (f32[4,1,1024]{2,1,0:T(1,128)S(1)}, f32[4,1,1024]{2,1,0:T(1,128)S(1)}, u32[]{:S(2)}, u32[]{:S(2)}) collective-permute-start(f32[4,1,1024]{2,1,0:T(1,128)S(1)} %get-tuple-element.40), channel_id=1, source_target_pairs={{0,1},{1,2},{2,3},{4,5},{5,6},{6,7},{8,9},{9,10},{10,11},{12,13},{... | collective-permute-start | bytes 49160 | tf_op jit(solution)/shard_map/ppermute | solution.py:15
  134.3 6.4 %collective-permute-start.33 = (f32[4,1,1024]{2,1,0:T(1,128)S(1)}, f32[4,1,1024]{2,1,0:T(1,128)S(1)}, u32[]{:S(2)}, u32[]{:S(2)}) collective-permute-start(f32[4,1,1024]{2,1,0:T(1,128)S(1)} %get-tuple-element.39), channel_id=1, source_target_pairs={{1,0},{2,1},{3,2},{5,4},{6,5},{7,6},{9,8},{10,9},{11,10},{13,12},{... | collective-permute-start | bytes 49160 | tf_op jit(solution)/shard_map/ppermute | solution.py:18
  135.6 5.7 %collective-permute-start.32 = (f32[4,1,1024]{2,1,0:T(1,128)S(1)}, f32[4,1,1024]{2,1,0:T(1,128)S(1)}, u32[]{:S(2)}, u32[]{:S(2)}) collective-permute-start(f32[4,1,1024]{2,1,0:T(1,128)S(1)} %get-tuple-element.38), channel_id=1, source_target_pairs={{0,1},{1,2},{2,3},{4,5},{5,6},{6,7},{8,9},{9,10},{10,11},{12,13},{... | collective-permute-start | bytes 49160 | tf_op jit(solution)/shard_map/ppermute | solution.py:15
  141.6 6.4 %collective-permute-start.35 = (f32[4,1,1024]{2,1,0:T(1,128)S(1)}, f32[4,1,1024]{2,1,0:T(1,128)S(1)}, u32[]{:S(2)}, u32[]{:S(2)}) collective-permute-start(f32[4,1,1024]{2,1,0:T(1,128)S(1)} %get-tuple-element.37), channel_id=1, source_target_pairs={{1,0},{2,1},{3,2},{5,4},{6,5},{7,6},{9,8},{10,9},{11,10},{13,12},{... | collective-permute-start | bytes 49160 | tf_op jit(solution)/shard_map/ppermute | solution.py:18
  142.9 5.7 %collective-permute-start.34 = (f32[4,1,1024]{2,1,0:T(1,128)S(1)}, f32[4,1,1024]{2,1,0:T(1,128)S(1)}, u32[]{:S(2)}, u32[]{:S(2)}) collective-permute-start(f32[4,1,1024]{2,1,0:T(1,128)S(1)} %get-tuple-element.36), channel_id=1, source_target_pairs={{0,1},{1,2},{2,3},{4,5},{5,6},{6,7},{8,9},{9,10},{10,11},{12,13},{... | collective-permute-start | bytes 49160 | tf_op jit(solution)/shard_map/ppermute | solution.py:15
  148.1 13.0 %copy-start.3 = (f32[8,4]{0,1:T(4,128)S(1)}, f32[8,4]{0,1:T(4,128)}, u32[]{:S(2)}) copy-start(f32[8,4]{0,1:T(4,128)} %param.15) | copy-start | bytes 388
  154.7 16.6 %all-to-all-start = ((f32[8,1,8192]{2,1,0:T(1,128)}), f32[8,1,8192]{2,1,0:T(1,128)S(1)}, u32[]{:S(2)}, u32[]{:S(2)}) async-start(f32[8,1,8192]{2,1,0:T(1,128)} %fusion.112), calls=%async_computation | async-start | bytes 524288 | tf_op jit(solution)/shard_map/all_to_all | solution.py:127
  190.1 50.6 %all-to-all-start.1 = ((f32[8,1,8192]{2,1,0:T(1,128)}), f32[8,1,8192]{2,1,0:T(1,128)S(1)}, u32[]{:S(2)}, u32[]{:S(2)}) async-start(f32[8,1,8192]{2,1,0:T(1,128)} %copy.66), calls=%async_computation.1 | async-start | bytes 524288 | tf_op jit(solution)/shard_map/all_to_all | solution.py:142
